TPU v7x, 256 devices: a whole 4x4x8 slice. The times are simulated.
256 devices in a mesh: row: 4 (over x), col: 16 (over z, core), depth: 4 (over y).
Axes of the slice: x: 4, y: 4, z: 8, core: 2. Of those that a mesh axis runs over, the one named last changes fastest.
Arguments:
- a_cols: float32 [32768, 1024], P(('row', 'col')), may hold values from -16 to 24, as said below
- past_panels: float32 [32768, 2048], P(('row', 'col'), 'depth'), may hold values from -1 to 1
Outputs:
- factor: float32 [32768, 1024], P(('row', 'col'))
Inputs may be any that keep to these rules, and one draw needn't show every extreme that they name: a_cols minus past_panels times the transpose of the top 1024 rows of past_panels is the first 1024 columns of a symmetric positive definite matrix whose top block has eigenvalues between 2 and 12.
All inputs are finite; a program needn't handle non-finite values.
Results may differ from a plain program's by a relative error of at most 0.0001.
Values sent between devices are 32-bit elements.
A program may use at most 64 MiB of HBM per device.

v0:
```python
import functools

import jax
import jax.numpy as jnp
from jax import lax
from jax.experimental import pallas as pl
from jax.experimental.pallas import tpu as pltpu
from jax.sharding import Mesh
from jax.sharding import PartitionSpec as P

W = 1024
B = 128
NBLK = W // B
PANEL = 16
AXES = ("row", "col_0", "col_1", "depth")
ROW_COL = ("row", "col_0", "col_1")
NT = (((1,), (1,)), ((), ()))
NN = (((1,), (0,)), ((), ()))
f32 = jnp.float32
bf16 = jnp.bfloat16
MESH = pl.DeviceIdType.MESH
VMEM = pl.BlockSpec(memory_space=pltpu.VMEM)


def tile_index(i, j):
    if i < 4:
        return i * (i + 1) // 2 + j
    if j < 4:
        return 10 + (i - 4) * 4 + j if i < 6 else 28 + (i - 6) * 4 + j
    return 18 + (i - 4) * (i - 3) // 2 + (j - 4)


def split(x):
    high = x.astype(bf16)
    return high, (x - high.astype(f32)).astype(bf16)


def dot3(a, b, dims=NT):
    dot = functools.partial(
        lax.dot_general, dimension_numbers=dims, preferred_element_type=f32
    )
    return dot(a[0], b[0]) + (dot(a[0], b[1]) + dot(a[1], b[0]))


def top_tiles(core, first, past_ref, other_ref, a_ref, tiles_ref):
    own = split(past_ref[...])
    square = dot3(own, own)

    def put(place, mat, value):
        tiles_ref[place * B : place * B + B, :] = jnp.where(first, mat, 0.0) - value

    def part(i, j):
        return slice(i * B, i * B + B), slice(j * B, j * B + B)

    @pl.when(core == 0)
    def _():
        for i in range(4):
            for j in range(i + 1):
                put(i * (i + 1) // 2 + j, a_ref[part(i, j)], square[part(i, j)])
        cross = dot3(split(other_ref[0:256, :]), own)
        for i in range(2):
            for j in range(4):
                put(10 + i * 4 + j, a_ref[part(j, 4 + i)].T, cross[part(i, j)])

    @pl.when(core == 1)
    def _():
        for i in range(4):
            for j in range(i + 1):
                put(i * (i + 1) // 2 + j, a_ref[part(i, 4 + j)], square[part(i, j)])
        cross = dot3(split(past_ref[256:512, :]), split(other_ref[...]))
        for i in range(2):
            for j in range(4):
                put(10 + i * 4 + j, a_ref[part(2 + i, j)], cross[part(i, j)])


def spread_kernel(
    past_ref, a_ref, so_ref, u_ref,
    to_ref, other_ref, tiles_ref, ybuf, th_ref, tl_ref, part_ref, half_ref, full_ref,
    sc_send_s, sc_send_t, sc_recv, y_send, y_recv,
    z_send, z_recv, x_send, x_recv, d_send, d_recv, r_send, r_recv, loc, swap,
):
    x = lax.axis_index("row")
    z = lax.axis_index("col_0")
    c = lax.axis_index("col_1")
    y = lax.axis_index("depth")
    me = x * 8 + z
    left = lax.rem(x + 3, 4)
    right = lax.rem(x + 1, 4)
    far = lax.rem(x + 2, 4)
    down = lax.rem(y + 3, 4)
    up = lax.rem(y + 1, 4)
    across = lax.rem(y + 2, 4)
    root = me == 0
    barrier = pltpu.get_barrier_semaphore()

    def greet(*device):
        pl.semaphore_signal(barrier, inc=1, device_id=device, device_id_type=MESH)

    def z_greet(k, carry):
        greet(x, lax.rem(z + k, 8), c, y)
        return carry

    lax.fori_loop(1, 8, z_greet, 0)
    for k in range(1, 4):
        greet(x, z, c, lax.rem(y + k, 4))
    greet(left, z, c, y)
    greet(right, z, c, y)
    greet(x, z, 1 - c, y)

    @pl.when(jnp.logical_not(root))
    def _():
        greet(0, 0, c, y)
        pl.semaphore_wait(barrier, 13)

    @pl.when(root)
    def _():
        pl.semaphore_wait(barrier, 44)

    def remote(src, dst, send, recv, *device):
        return pltpu.make_async_remote_copy(
            src_ref=src, dst_ref=dst, send_sem=send, recv_sem=recv,
            device_id=device, device_id_type=MESH,
        )

    size = (72, 16)
    full = (so_ref, to_ref)
    pair = (1, 0)

    def pieces(n, core, start, count):
        rows = size[n]
        return full[n].at[pl.ds(pl.multiple_of((core * 32 + start) * rows, 8), count * rows)]

    def source(n, q):
        ref = (tiles_ref, past_ref)[n]
        return ref.at[pl.ds(pl.multiple_of(q * size[n], 8), size[n])]

    def scatter(n, q):
        dst = ybuf.at[y] if n == 0 else pieces(1, c, q, 1)
        send = (sc_send_s, sc_send_t)[n]
        return remote(source(n, q), dst, send.at[q], sc_recv.at[n], q // 8, lax.rem(q, 8), c, y)

    def scatter_all(n):
        def go(q, carry):
            scatter(n, q).start()
            return carry

        lax.fori_loop(1, 32, go, 0)

    def scatter_wait(n):
        dst = ybuf.at[y] if n == 0 else pieces(1, c, me, 1)
        send = (sc_send_s, sc_send_t)[n]
        remote(source(n, 0), dst, send.at[0], sc_recv.at[n], 0, 0, c, y).wait_recv()

    def z_copy(n, k):
        mine = pieces(n, c, me, 1)
        return remote(mine, mine, z_send.at[n, k], z_recv.at[n, z], x, lax.rem(z + k, 8), c, y)

    def z_start(n):
        def go(k, carry):
            z_copy(n, k).start()
            return carry

        lax.fori_loop(1, 8, go, 0)

    def z_wait(n):
        def wait(k, carry):
            peer = lax.rem(z + k, 8)
            slot = pieces(n, c, x * 8 + peer, 1)
            remote(slot, slot, z_send.at[n, 0], z_recv.at[n, peer], x, peer, c, y).wait_recv()
            return carry

        lax.fori_loop(1, 8, wait, 0)

    def group(n, core, g):
        return pieces(n, core, g * 8, 8)

    def half(n, g, h):
        return pieces(n, c, g * 8 + h * 4, 4)

    def x_copy(n, d):
        mine = group(n, c, x)
        return remote(mine, mine, x_send.at[n, d], x_recv.at[n, d], (right, left)[d], z, c, y)

    def x_wait(n, d):
        g = (left, right)[d]
        slot = group(n, c, g)
        remote(slot, slot, x_send.at[n, d], x_recv.at[n, d], g, z, c, y).wait_recv()

    def relay(n, d):
        part = half(n, (left, right)[d], d)
        return remote(part, part, x_send.at[n, 2 + d], x_recv.at[n, 2 + d], (right, left)[d], z, c, y)

    def relay_wait(n, d):
        slot = half(n, far, d)
        remote(slot, slot, x_send.at[n, 2 + d], x_recv.at[n, 2 + d], (left, right)[d], z, c, y).wait_recv()

    order = (x, left, right, far)

    def cross(n, k):
        slot = group(n, c, order[k])
        return remote(slot, slot, d_send.at[n, k], d_recv.at[n, k], x, z, 1 - c, y)

    def cross_wait(n, k):
        slot = group(n, 1 - c, order[k])
        remote(slot, slot, d_send.at[n, k], d_recv.at[n, k], x, z, 1 - c, y).wait_recv()

    trade = remote(past_ref, other_ref, swap.at[0], swap.at[1], x, z, 1 - c, y)
    own_t = pltpu.make_async_copy(source(1, 0), pieces(1, c, 0, 1), loc.at[0])
    own_s = pltpu.make_async_copy(source(0, 0), ybuf.at[y], loc.at[1])

    @pl.when(root)
    def _():
        trade.start()
        own_t.start()
        scatter_all(1)
        own_t.wait()
        z_start(1)
        trade.wait_recv()
        top_tiles(c, y == 0, past_ref, other_ref, a_ref, tiles_ref)
        own_s.start()
        scatter_all(0)
        own_s.wait()

    @pl.when(jnp.logical_not(root))
    def _():
        scatter_wait(1)
        z_start(1)

    z_wait(1)
    for d in range(2):
        x_copy(1, d).start()
    cross(1, 0).start()

    @pl.when(jnp.logical_not(root))
    def _():
        scatter_wait(0)

    def y_copy(k):
        return remote(ybuf.at[y], ybuf.at[y], y_send.at[k], y_recv.at[y], x, z, c, lax.rem(y + k, 4))

    for k in range(1, 4):
        y_copy(k).start()
    for d in range(2):
        x_wait(1, d)
        relay(1, d).start()
        cross(1, 1 + d).start()
    for k in range(1, 4):
        peer = lax.rem(y + k, 4)
        slot = ybuf.at[peer]
        remote(slot, slot, y_send.at[0], y_recv.at[peer], x, z, c, peer).wait_recv()
    so_ref[pl.ds(pl.multiple_of((c * 32 + me) * 72, 8), 72), :] = (ybuf[0] + ybuf[1]) + (ybuf[2] + ybuf[3])
    z_start(0)
    for d in range(2):
        relay_wait(1, d)
    cross(1, 3).start()
    for k in range(4):
        cross_wait(1, k)

    th_ref[...], tl_ref[...] = split(to_ref[...])

    def update(k):
        at = pl.multiple_of(lax.rem(y + k, 4) * B, B)
        mine = split(past_ref[pl.ds(at, B), :])
        for n in range(2):
            cols = slice(n * 512, n * 512 + 512)
            part_ref[k, :, cols] = dot3(mine, (th_ref[cols, :], tl_ref[cols, :]))

    def reduce_first(d):
        rows = pl.ds(d * 64, 64)
        return remote(part_ref.at[2, rows], half_ref.at[d], r_send.at[d], r_recv.at[d], x, z, c, (up, down)[d])

    def reduce_own(d):
        rows = pl.ds(64 - d * 64, 64)
        return remote(
            part_ref.at[1 + 2 * d, rows], full_ref.at[d, rows], r_send.at[2 + d], r_recv.at[2 + d],
            x, z, c, (up, down)[d],
        )

    def reduce_sum(d):
        rows = pl.ds(d * 64, 64)
        return remote(
            part_ref.at[1 + 2 * d, rows], full_ref.at[d, rows], r_send.at[4 + d], r_recv.at[4 + d],
            x, z, c, (up, down)[d],
        )

    update(2)
    for d in range(2):
        reduce_first(d).start()
    for d in range(2):
        update(1 + 2 * d)
        reduce_own(d).start()
    z_wait(0)
    for d in range(2):
        x_copy(0, d).start()
    cross(0, 0).start()
    update(0)
    for d in range(2):
        reduce_first(d).wait_recv()
        rows = slice(d * 64, d * 64 + 64)
        part_ref[1 + 2 * d, rows, :] += half_ref[d]
        reduce_sum(d).start()
    for d in range(2):
        x_wait(0, d)
        relay(0, d).start()
        cross(0, 1 + d).start()
    for d in range(2):
        relay_wait(0, d)
    cross(0, 3).start()
    for k in range(4):
        cross_wait(0, k)
    for d in range(2):
        reduce_own(d).wait_recv()
        reduce_sum(d).wait_recv()
    at = pl.multiple_of(y * B, B)
    u_ref[...] = a_ref[pl.ds(at, B), :] - (part_ref[0] + (full_ref[0] + full_ref[1]))

    @pl.when(root)
    def _():
        trade.wait_send()

        def done(q, carry):
            scatter(0, q).wait_send()
            scatter(1, q).wait_send()
            return carry

        lax.fori_loop(1, 32, done, 0)

    for k in range(1, 4):
        y_copy(k).wait_send()
    for n in pair:
        def done_z(k, carry):
            z_copy(n, k).wait_send()
            return carry

        lax.fori_loop(1, 8, done_z, 0)
        for d in range(2):
            x_copy(n, d).wait_send()
            relay(n, d).wait_send()
        for k in range(4):
            cross(n, k).wait_send()
    for d in range(2):
        reduce_first(d).wait_send()
        reduce_own(d).wait_send()
        reduce_sum(d).wait_send()


def spread(past, a_cols):
    dma = pltpu.SemaphoreType.DMA
    return pl.pallas_call(
        spread_kernel,
        out_shape=(
            jax.ShapeDtypeStruct((36 * B, B), f32),
            jax.ShapeDtypeStruct((B, W), f32),
        ),
        in_specs=[VMEM] * 2,
        out_specs=(VMEM, VMEM),
        scratch_shapes=[
            pltpu.VMEM((W, 512), f32),
            pltpu.VMEM((512, 512), f32),
            pltpu.VMEM((18 * B, B), f32),
            pltpu.VMEM((4, 72, B), f32),
            pltpu.VMEM((W, 512), bf16),
            pltpu.VMEM((W, 512), bf16),
            pltpu.VMEM((4, B, W), f32),
            pltpu.VMEM((2, 64, W), f32),
            pltpu.VMEM((2, B, W), f32),
            dma((32,)), dma((32,)), dma((2,)), dma((4,)), dma((4,)),
            dma((2, 8)), dma((2, 8)), dma((2, 4)), dma((2, 4)), dma((2, 4)), dma((2, 4)),
            dma((6,)), dma((6,)), dma((2,)), dma((2,)),
        ],
        compiler_params=pltpu.CompilerParams(collective_id=0, has_side_effects=True),
        name="spread",
    )(past, a_cols)


def row_of(v, m):
    return jnp.broadcast_to(v[m : m + 1, :], v.shape)


def inverse_factor(w, fill):
    lane = lax.broadcasted_iota(jnp.int32, (8, B), 1)
    sub = lax.broadcasted_iota(jnp.int32, (8, B), 0)
    k, kg, n = PANEL, PANEL // 8, B // 8
    w = list(w)
    for t in range(B // k):
        r0, g0 = t * k, t * kg
        cols = [
            [jnp.broadcast_to(w[g][:, r0 + m : r0 + m + 1], (8, B)) for g in range(g0, n)]
            for m in range(k)
        ]
        in_panel = (lane >= r0) & (lane < r0 + k)
        for g in range(g0, n):
            unit = jnp.where(lane == sub + 8 * g, 1.0, 0.0) if g < g0 + kg else jnp.zeros((8, B), f32)
            w[g] = jnp.where(in_panel, unit, w[g])
        piv = [[cols[m][g] for g in range(kg)] for m in range(k)]
        rows = [w[g0 + g] for g in range(kg)]
        final = [None] * k
        for m in range(k):
            gm, sm = divmod(m, 8)
            inv = lax.rsqrt(row_of(piv[m][gm], sm))
            inv2 = inv * inv
            row = row_of(rows[gm], sm)
            final[m] = row * inv
            step = row * inv2
            for g in range(kg):
                new = rows[g] - piv[m][g] * step
                rows[g] = jnp.where(sub == sm, step, new) if g == gm else new
            for m2 in range(m + 1, k):
                f = row_of(piv[m2][gm], sm) * inv2
                for g in range(kg):
                    new = piv[m2][g] - piv[m][g] * f
                    piv[m2][g] = jnp.where(sub == sm, f, new) if g == gm else new
        for g in range(kg):
            acc = final[8 * g]
            for s in range(1, 8):
                acc = jnp.where(sub == s, final[8 * g + s], acc)
            w[g0 + g] = acc
        spread_rows = [row_of(rows[m // 8], m % 8) for m in range(k)]
        for g in range(g0 + kg, n):
            acc = w[g]
            for m in range(k):
                acc = acc - cols[m][g - g0] * spread_rows[m]
            w[g] = acc
        fill(t)
    return [jnp.where(lane <= sub + 8 * g, w[g], 0.0) for g in range(n)]


def factor_kernel(s_ref, lh_ref, ll_ref, dh_ref, dl_ref, a_ref):
    def rows(i, n=1):
        return slice(i * B, (i + n) * B)

    for i in range(NBLK):
        for j in range(i + 1):
            a_ref[rows(i), rows(j)] = s_ref[tile_index(i, j)]

    def low(i, n, j):
        return lh_ref[rows(i, n), rows(j)], ll_ref[rows(i, n), rows(j)]

    def panel(i, n, s, d):
        high, lo = split(dot3(split(a_ref[rows(i, n), rows(s)]), d))
        lh_ref[rows(i, n), rows(s)] = high
        ll_ref[rows(i, n), rows(s)] = lo

    def trail(i, n, j, nj, s):
        a_ref[rows(i, n), rows(j, nj)] -= dot3(low(i, n, s), low(j, nj, s))

    waiting = []
    halves = [None, None]
    for s in range(NBLK):
        def fill(t):
            n = -(-len(waiting) // (8 - t))
            for _ in range(n):
                waiting.pop(0)()

        w = [a_ref[s * B + 8 * g : s * B + 8 * g + 8, rows(s)] for g in range(16)]
        w = inverse_factor(w, fill)
        d32 = jnp.concatenate(w, axis=0)
        d = split(d32)
        halves[s % 2] = d
        at = (s % 2) * B
        dh_ref[s // 2, at : at + B, at : at + B] = d[0]
        dl_ref[s // 2, at : at + B, at : at + B] = d[1]
        if s % 2 == 0:
            dh_ref[s // 2, 0:B, B : 2 * B] = jnp.zeros((B, B), bf16)
            dl_ref[s // 2, 0:B, B : 2 * B] = jnp.zeros((B, B), bf16)
        if s + 1 < NBLK:
            panel(s + 1, 1, s, d)
            trail(s + 1, 1, s + 1, 1, s)
        if s + 2 < NBLK:
            def rest(s=s, d=d):
                panel(s + 2, NBLK - s - 2, s, d)

            waiting.append(rest)
            waiting.append(functools.partial(trail, s + 2, NBLK - s - 2, s + 1, 1, s))
            for j in range(s + 2, NBLK):
                waiting.append(functools.partial(trail, j, NBLK - j, j, 1, s))
        if s % 2 == 1:
            def corner(s=s, first=halves[0], second=halves[1]):
                mid = dot3(low(s, 1, s - 1), first, NN)
                high, lo = split(-dot3(second, split(mid), NN))
                dh_ref[s // 2, B : 2 * B, 0:B] = high
                dl_ref[s // 2, B : 2 * B, 0:B] = lo

            waiting.append(corner)
    for job in waiting:
        job()


def factor_top(tiles):
    return pl.pallas_call(
        factor_kernel,
        out_shape=(
            jax.ShapeDtypeStruct((W, W), bf16),
            jax.ShapeDtypeStruct((W, W), bf16),
            jax.ShapeDtypeStruct((4, 256, 256), bf16),
            jax.ShapeDtypeStruct((4, 256, 256), bf16),
        ),
        in_specs=[VMEM],
        out_specs=(VMEM,) * 4,
        scratch_shapes=[pltpu.VMEM((W, W), f32)],
        cost_estimate=pl.CostEstimate(flops=10**11, bytes_accessed=7 * 2**20, transcendentals=0),
        name="factor_top",
    )(tiles)


def solve_kernel(u0, u1, u2, u3, lh_ref, ll_ref, dh_ref, dl_ref, out_ref, acc, xh, xl):
    depth = lax.axis_index("depth")
    x, z, c = (lax.axis_index(a) for a in ROW_COL)
    base = (x * 16 + z * 2 + c) * 512
    for q, u in enumerate((u0, u1, u2, u3)):
        acc[q * B : q * B + B, :] = u[...]
    for n in range(4):
        cols = slice(n * 256, n * 256 + 256)
        u = acc[:, cols]
        if n:
            done = slice(0, n * 256)
            u = u - dot3((xh[:, done], xl[:, done]), (lh_ref[cols, done], ll_ref[cols, done]))
        out = dot3(split(u), (dh_ref[n], dl_ref[n]))
        xh[:, cols], xl[:, cols] = split(out)
        col = lax.broadcasted_iota(jnp.int32, (B, 256), 1) + n * 256
        for q in range(4):
            place = pl.multiple_of(lax.rem(depth + 4 - q, 4) * B, B)
            row = lax.broadcasted_iota(jnp.int32, (B, 256), 0) + (base + place)
            out_ref[pl.ds(place, B), cols] = jnp.where(row >= col, out[q * B : q * B + B, :], 0.0)


def solve(parts, lower):
    return pl.pallas_call(
        solve_kernel,
        out_shape=jax.ShapeDtypeStruct((512, W), f32),
        in_specs=[VMEM] * 8,
        out_specs=VMEM,
        scratch_shapes=[pltpu.VMEM((512, W), f32), pltpu.VMEM((512, W), bf16), pltpu.VMEM((512, W), bf16)],
        name="solve",
    )(*parts, *lower)


def shift(value, k):
    return lax.ppermute(value, "depth", [(i, (i + k) % 4) for i in range(4)])


def body(a_cols, past):
    tiles, mine = spread(past, a_cols)
    parts = [mine] + [shift(mine, k) for k in range(1, 4)]
    lower = factor_top(tiles.reshape(36, B, B))
    return solve(parts, lower)


def solution(mesh):
    split_mesh = Mesh(
        mesh.devices.reshape(mesh.shape["row"], 8, 2, mesh.shape["depth"]), AXES
    )
    placed = (P(ROW_COL, None), P(ROW_COL, "depth"))
    return jax.shard_map(
        body, mesh=split_mesh, in_specs=placed, out_specs=P(ROW_COL, None), check_vma=False
    )
```

profile of v0, /device:TPU:1, one launch (start us, length us, event | category | flops | bytes accessed | tf_op | source)
XLA Modules:
  0.0 125.6 jit_solution(5723794595504275332)
XLA Ops:
  0.0 75.8 %spread.1 = (f32[4608,128]{1,0:T(8,128)}, f32[128,1024]{1,0:T(8,128)}) custom-call(f32[512,512]{1,0:T(8,128)} %past_ref.1, f32[512,1024]{1,0:T(8,128)} %a_ref.1), custom_call_target="tpu_custom_call" | custom-call | tf_op jit(solution)/shard_map/spread/pallas_call | solution.py:349
  75.8 0.1 collective-permute-start
  75.9 1.5 %collective-permute-start.1 = (f32[128,1024]{1,0:T(8,128)}, f32[128,1024]{1,0:T(8,128)S(1)}, u32[]{:S(2)}, u32[]{:S(2)}) collective-permute-start(f32[128,1024]{1,0:T(8,128)} %get-tuple-element.11.u0), channel_id=1, source_target_pairs={{0,2},{1,3},{2,0},{3,1},{4,6},{5,7},{6,4},{7,5},{8,10},{9,11},{10,... | collective-permute-start | bytes 1572872 | tf_op jit(solution)/shard_map/ppermute | solution.py:539
  77.4 1.8 %collective-permute-start.2 = (f32[128,1024]{1,0:T(8,128)}, f32[128,1024]{1,0:T(8,128)S(1)}, u32[]{:S(2)}, u32[]{:S(2)}) collective-permute-start(f32[128,1024]{1,0:T(8,128)} %get-tuple-element.11.u0), channel_id=1, source_target_pairs={{0,3},{1,0},{2,1},{3,2},{4,7},{5,4},{6,5},{7,6},{8,11},{9,8},{10,9... | collective-permute-start | bytes 1572872 | tf_op jit(solution)/shard_map/ppermute | solution.py:539
  79.2 36.8 %factor_top.1 = (bf16[1024,1024]{1,0:T(8,128)(2,1)}, bf16[1024,1024]{1,0:T(8,128)(2,1)}, bf16[4,256,256]{2,1,0:T(8,128)(2,1)}, bf16[4,256,256]{2,1,0:T(8,128)(2,1)}) custom-call(f32[36,128,128]{2,1,0:T(8,128)} %bitcast.1), custom_call_target="tpu_custom_call" | custom-call | flops 99999997952 | bytes 7340032 | tf_op jit(solution)/shard_map/factor_top/pallas_call | solution.py:490
  116.0 0.0 collective-permute-done.u1
  116.0 0.0 copy-start
  116.0 0.0 collective-permute-done.1.u2
  116.0 0.0 copy-start.1
  116.0 0.0 collective-permute-done.2.u3
  116.0 0.0 copy-start.2
  116.0 0.8 copy-done
  116.8 0.2 copy-done.1
  117.0 0.2 copy-done.2
  117.2 8.4 %solve.1 = f32[512,1024]{1,0:T(8,128)} custom-call(f32[128,1024]{1,0:T(8,128)} %get-tuple-element.11.u0, f32[128,1024]{1,0:T(8,128)} %copy-done, f32[128,1024]{1,0:T(8,128)} %copy-done.1, f32[128,1024]{1,0:T(8,128)} %copy-done.2, bf16[1024,1024]{1,0:T(8,128)(2,1)} %get-tuple-element.13.lh_ref, bf16[1024,1024]{1,0:T(8,128)(2,1)} %get-tuple-element.14.ll_ref, ...), custom_call_target="tpu_custom_call" | custom-call | tf_op jit(solution)/shard_map/solve/pallas_call | solution.py:528
Async XLA Ops:
  75.8 40.2 %collective-permute-start = (f32[128,1024]{1,0:T(8,128)}, f32[128,1024]{1,0:T(8,128)S(1)}, u32[]{:S(2)}, u32[]{:S(2)}) collective-permute-start(f32[128,1024]{1,0:T(8,128)} %get-tuple-element.11.u0), channel_id=1, source_target_pairs={{0,1},{1,2},{2,3},{3,0},{4,5},{5,6},{6,7},{7,4},{8,9},{9,10},{10,1... | collective-permute-start | bytes 1572872 | tf_op jit(solution)/shard_map/ppermute | solution.py:539
  75.9 40.2 %collective-permute-start.1 = (f32[128,1024]{1,0:T(8,128)}, f32[128,1024]{1,0:T(8,128)S(1)}, u32[]{:S(2)}, u32[]{:S(2)}) collective-permute-start(f32[128,1024]{1,0:T(8,128)} %get-tuple-element.11.u0), channel_id=1, source_target_pairs={{0,2},{1,3},{2,0},{3,1},{4,6},{5,7},{6,4},{7,5},{8,10},{9,11},{10,... | collective-permute-start | bytes 1572872 | tf_op jit(solution)/shard_map/ppermute | solution.py:539
  77.4 38.6 %collective-permute-start.2 = (f32[128,1024]{1,0:T(8,128)}, f32[128,1024]{1,0:T(8,128)S(1)}, u32[]{:S(2)}, u32[]{:S(2)}) collective-permute-start(f32[128,1024]{1,0:T(8,128)} %get-tuple-element.11.u0), channel_id=1, source_target_pairs={{0,3},{1,0},{2,1},{3,2},{4,7},{5,4},{6,5},{7,6},{8,11},{9,8},{10,9... | collective-permute-start | bytes 1572872 | tf_op jit(solution)/shard_map/ppermute | solution.py:539
  116.0 0.8 copy-start
  116.0 1.0 copy-start.1
  116.0 1.1 copy-start.2
where the time goes:
time: 127 us; the launch traced here: 126 us
  Pallas kernels  121 us (95%)
  starting transfers between devices  3.44 us (3%)
    pallas_call x1, Pallas kernels, spread(): pl.pallas_call(spread_kernel, out_shape=(jax.ShapeDtypeStruct((36 * B, B)...  75.8 us
    pallas_call x1, Pallas kernels, factor_top(): pl.pallas_call(factor_kernel, out_shape=(jax.ShapeDtypeStruct((W, W), bf1...  36.8 us
    pallas_call x1, Pallas kernels, solve(): pl.pallas_call(solve_kernel, out_shape=jax.ShapeDtypeStruct((512, W), f32...  8.44 us
    ppermute x3, starting transfers between devices, shift(): return lax.ppermute(value, 'depth', [(i, (i + k) % 4) for i in range(4)])  3.44 us
  transfers between devices with their start and end apart: 3, of which 0 were waited for; matrix products, arithmetic and copies ran while one was open for 0% of the time, Pallas kernels for 29%

commit v1 on v0

--- a/solution.py
+++ b/solution.py
@@ -73,8 +73,9 @@
                 put(10 + i * 4 + j, a_ref[part(2 + i, j)], cross[part(i, j)])
 
 
-def spread_kernel(
-    past_ref, a_ref, so_ref, u_ref,
+def whole_kernel(
+    past_ref, a_ref, out_ref,
+    so_ref, u_ref, top_ref, lh_ref, ll_ref, dh_ref, dl_ref, xh_ref, xl_ref, g_send, g_recv,
     to_ref, other_ref, tiles_ref, ybuf, th_ref, tl_ref, part_ref, half_ref, full_ref,
     sc_send_s, sc_send_t, sc_recv, y_send, y_recv,
     z_send, z_recv, x_send, x_recv, d_send, d_recv, r_send, r_recv, loc, swap,
@@ -312,7 +313,29 @@
         reduce_own(d).wait_recv()
         reduce_sum(d).wait_recv()
     at = pl.multiple_of(y * B, B)
-    u_ref[...] = a_ref[pl.ds(at, B), :] - (part_ref[0] + (full_ref[0] + full_ref[1]))
+    u_ref[0:B, :] = a_ref[pl.ds(at, B), :] - (part_ref[0] + (full_ref[0] + full_ref[1]))
+
+    def gather(d):
+        to = pl.ds((1 + 2 * d) * B, B)
+        return remote(u_ref.at[pl.ds(0, B)], u_ref.at[to], g_send.at[d], g_recv.at[d], x, z, c, (up, down)[d])
+
+    def gather_on(d):
+        mine = pl.ds((1 + 2 * d) * B + d * 64, 64)
+        to = pl.ds(2 * B + d * 64, 64)
+        return remote(u_ref.at[mine], u_ref.at[to], g_send.at[2 + d], g_recv.at[2 + d], x, z, c, (up, down)[d])
+
+    for d in range(2):
+        gather(d).start()
+
+    def pass_on():
+        for d in range(2):
+            gather(d).wait_recv()
+            gather_on(d).start()
+
+    factor_top(so_ref, lh_ref, ll_ref, dh_ref, dl_ref, top_ref, {4: pass_on})
+    for d in range(2):
+        gather_on(d).wait_recv()
+    solve(y, (x * 16 + z * 2 + c) * 512, u_ref, lh_ref, ll_ref, dh_ref, dl_ref, out_ref, xh_ref, xl_ref)
 
     @pl.when(root)
     def _():
@@ -342,19 +365,28 @@
         reduce_first(d).wait_send()
         reduce_own(d).wait_send()
         reduce_sum(d).wait_send()
-
-
-def spread(past, a_cols):
+        gather(d).wait_send()
+        gather_on(d).wait_send()
+
+
+def whole(past, a_cols):
     dma = pltpu.SemaphoreType.DMA
     return pl.pallas_call(
-        spread_kernel,
-        out_shape=(
-            jax.ShapeDtypeStruct((36 * B, B), f32),
-            jax.ShapeDtypeStruct((B, W), f32),
-        ),
+        whole_kernel,
+        out_shape=jax.ShapeDtypeStruct((512, W), f32),
         in_specs=[VMEM] * 2,
-        out_specs=(VMEM, VMEM),
+        out_specs=VMEM,
         scratch_shapes=[
+            pltpu.VMEM((36 * B, B), f32),
+            pltpu.VMEM((4 * B, W), f32),
+            pltpu.VMEM((W, W), f32),
+            pltpu.VMEM((W, W), bf16),
+            pltpu.VMEM((W, W), bf16),
+            pltpu.VMEM((4, 256, 256), bf16),
+            pltpu.VMEM((4, 256, 256), bf16),
+            pltpu.VMEM((4 * B, W), bf16),
+            pltpu.VMEM((4 * B, W), bf16),
+            dma((4,)), dma((4,)),
             pltpu.VMEM((W, 512), f32),
             pltpu.VMEM((512, 512), f32),
             pltpu.VMEM((18 * B, B), f32),
@@ -369,69 +401,55 @@
             dma((6,)), dma((6,)), dma((2,)), dma((2,)),
         ],
         compiler_params=pltpu.CompilerParams(collective_id=0, has_side_effects=True),
-        name="spread",
+        name="whole",
     )(past, a_cols)
 
 
-def row_of(v, m):
-    return jnp.broadcast_to(v[m : m + 1, :], v.shape)
-
-
 def inverse_factor(w, fill):
-    lane = lax.broadcasted_iota(jnp.int32, (8, B), 1)
-    sub = lax.broadcasted_iota(jnp.int32, (8, B), 0)
-    k, kg, n = PANEL, PANEL // 8, B // 8
-    w = list(w)
+    lane = lax.broadcasted_iota(jnp.int32, (B, B), 1)
+    sub = lax.broadcasted_iota(jnp.int32, (B, B), 0)
+    k = PANEL
+    at = sub[:k]
+    done = []
     for t in range(B // k):
-        r0, g0 = t * k, t * kg
-        cols = [
-            [jnp.broadcast_to(w[g][:, r0 + m : r0 + m + 1], (8, B)) for g in range(g0, n)]
-            for m in range(k)
-        ]
-        in_panel = (lane >= r0) & (lane < r0 + k)
-        for g in range(g0, n):
-            unit = jnp.where(lane == sub + 8 * g, 1.0, 0.0) if g < g0 + kg else jnp.zeros((8, B), f32)
-            w[g] = jnp.where(in_panel, unit, w[g])
-        piv = [[cols[m][g] for g in range(kg)] for m in range(k)]
-        rows = [w[g0 + g] for g in range(kg)]
-        final = [None] * k
+        r0 = t * k
+        left = B - r0
+        cols = [jnp.broadcast_to(w[:, r0 + m : r0 + m + 1], (left, B)) for m in range(k)]
+        lanes, subs = lane[:left], sub[:left]
+        unit = jnp.where((lanes == subs + r0) & (subs < k), 1.0, 0.0)
+        w = jnp.where((lanes >= r0) & (lanes < r0 + k), unit, w)
+        rows = w[:k]
+        piv = jnp.stack([col[:k] for col in cols])
+        final = jnp.zeros((k, B), f32)
         for m in range(k):
-            gm, sm = divmod(m, 8)
-            inv = lax.rsqrt(row_of(piv[m][gm], sm))
+            mine, rest = piv[0], piv[1:]
+            inv = lax.rsqrt(jnp.broadcast_to(mine[m : m + 1], (k, B)))
             inv2 = inv * inv
-            row = row_of(rows[gm], sm)
-            final[m] = row * inv
+            row = jnp.broadcast_to(rows[m : m + 1], (k, B))
+            here = at == m
+            final = jnp.where(here, row * inv, final)
             step = row * inv2
-            for g in range(kg):
-                new = rows[g] - piv[m][g] * step
-                rows[g] = jnp.where(sub == sm, step, new) if g == gm else new
-            for m2 in range(m + 1, k):
-                f = row_of(piv[m2][gm], sm) * inv2
-                for g in range(kg):
-                    new = piv[m2][g] - piv[m][g] * f
-                    piv[m2][g] = jnp.where(sub == sm, f, new) if g == gm else new
-        for g in range(kg):
-            acc = final[8 * g]
-            for s in range(1, 8):
-                acc = jnp.where(sub == s, final[8 * g + s], acc)
-            w[g0 + g] = acc
-        spread_rows = [row_of(rows[m // 8], m % 8) for m in range(k)]
-        for g in range(g0 + kg, n):
-            acc = w[g]
+            rows = jnp.where(here, step, rows - mine * step)
+            if m + 1 < k:
+                f = jnp.broadcast_to(rest[:, m : m + 1], (k - 1 - m, k, B)) * inv2[None]
+                piv = jnp.where(here[None], f, rest - mine[None] * f)
+        done.append(jnp.where(lane[:k] <= at + r0, final, 0.0))
+        if left > k:
+            w = w[k:]
             for m in range(k):
-                acc = acc - cols[m][g - g0] * spread_rows[m]
-            w[g] = acc
+                w = w - cols[m][k:] * jnp.broadcast_to(rows[m : m + 1], (left - k, B))
         fill(t)
-    return [jnp.where(lane <= sub + 8 * g, w[g], 0.0) for g in range(n)]
-
-
-def factor_kernel(s_ref, lh_ref, ll_ref, dh_ref, dl_ref, a_ref):
+    return jnp.concatenate(done, axis=0)
+
+
+def factor_top(s_ref, lh_ref, ll_ref, dh_ref, dl_ref, a_ref, events):
     def rows(i, n=1):
         return slice(i * B, (i + n) * B)
 
     for i in range(NBLK):
         for j in range(i + 1):
-            a_ref[rows(i), rows(j)] = s_ref[tile_index(i, j)]
+            n = tile_index(i, j)
+            a_ref[rows(i), rows(j)] = s_ref[rows(n), :]
 
     def low(i, n, j):
         return lh_ref[rows(i, n), rows(j)], ll_ref[rows(i, n), rows(j)]
@@ -448,14 +466,13 @@
     halves = [None, None]
     for s in range(NBLK):
         def fill(t):
-            n = -(-len(waiting) // (8 - t))
+            n = -(-len(waiting) // (B // PANEL - t))
             for _ in range(n):
                 waiting.pop(0)()
 
-        w = [a_ref[s * B + 8 * g : s * B + 8 * g + 8, rows(s)] for g in range(16)]
-        w = inverse_factor(w, fill)
-        d32 = jnp.concatenate(w, axis=0)
-        d = split(d32)
+        if s in events:
+            waiting.append(events[s])
+        d = split(inverse_factor(a_ref[rows(s), rows(s)], fill))
         halves[s % 2] = d
         at = (s % 2) * B
         dh_ref[s // 2, at : at + B, at : at + B] = d[0]
@@ -486,32 +503,10 @@
         job()
 
 
-def factor_top(tiles):
-    return pl.pallas_call(
-        factor_kernel,
-        out_shape=(
-            jax.ShapeDtypeStruct((W, W), bf16),
-            jax.ShapeDtypeStruct((W, W), bf16),
-            jax.ShapeDtypeStruct((4, 256, 256), bf16),
-            jax.ShapeDtypeStruct((4, 256, 256), bf16),
-        ),
-        in_specs=[VMEM],
-        out_specs=(VMEM,) * 4,
-        scratch_shapes=[pltpu.VMEM((W, W), f32)],
-        cost_estimate=pl.CostEstimate(flops=10**11, bytes_accessed=7 * 2**20, transcendentals=0),
-        name="factor_top",
-    )(tiles)
-
-
-def solve_kernel(u0, u1, u2, u3, lh_ref, ll_ref, dh_ref, dl_ref, out_ref, acc, xh, xl):
-    depth = lax.axis_index("depth")
-    x, z, c = (lax.axis_index(a) for a in ROW_COL)
-    base = (x * 16 + z * 2 + c) * 512
-    for q, u in enumerate((u0, u1, u2, u3)):
-        acc[q * B : q * B + B, :] = u[...]
+def solve(depth, base, u_ref, lh_ref, ll_ref, dh_ref, dl_ref, out_ref, xh, xl):
     for n in range(4):
         cols = slice(n * 256, n * 256 + 256)
-        u = acc[:, cols]
+        u = u_ref[:, cols]
         if n:
             done = slice(0, n * 256)
             u = u - dot3((xh[:, done], xl[:, done]), (lh_ref[cols, done], ll_ref[cols, done]))
@@ -524,26 +519,8 @@
             out_ref[pl.ds(place, B), cols] = jnp.where(row >= col, out[q * B : q * B + B, :], 0.0)
 
 
-def solve(parts, lower):
-    return pl.pallas_call(
-        solve_kernel,
-        out_shape=jax.ShapeDtypeStruct((512, W), f32),
-        in_specs=[VMEM] * 8,
-        out_specs=VMEM,
-        scratch_shapes=[pltpu.VMEM((512, W), f32), pltpu.VMEM((512, W), bf16), pltpu.VMEM((512, W), bf16)],
-        name="solve",
-    )(*parts, *lower)
-
-
-def shift(value, k):
-    return lax.ppermute(value, "depth", [(i, (i + k) % 4) for i in range(4)])
-
-
 def body(a_cols, past):
-    tiles, mine = spread(past, a_cols)
-    parts = [mine] + [shift(mine, k) for k in range(1, 4)]
-    lower = factor_top(tiles.reshape(36, B, B))
-    return solve(parts, lower)
+    return whole(past, a_cols)
 
 
 def solution(mesh):

time: 127 us -> 109 us (0.86)
  Pallas kernels: 121 us -> 105 us
  starting transfers between devices: 3.44 us -> 0 us
  local copies, waits for them, and re-layouts: 1.11 us -> 3.16 us
    pallas_call x3 -> x1, Pallas kernels: 121 us -> 105 us  [whole(): pl.pallas_call(whole_kernel, out_shape=jax.ShapeDtypeStruct((512, W), f32...]
    ppermute x3 -> x0, starting transfers between devices: 3.44 us -> none  [shift(): return lax.ppermute(value, 'depth', [(i, (i + k) % 4) for i in range(4)])]
    unnamed x6 -> x1, local copies, waits for them, and re-layouts: 1.11 us -> 3.16 us
  transfers between devices with their start and end apart: 3 -> 0, of which waited for: 0 -> 0; matrix products, arithmetic and copies ran while one was open for 0% -> 0% of each run, Pallas kernels for 29% -> 0%
where the time goes in v1:
time: 109 us; the launch traced here: 108 us
  Pallas kernels  105 us (96%)
  local copies, waits for them, and re-layouts  3.16 us (3%)
    pallas_call x1, Pallas kernels, whole(): pl.pallas_call(whole_kernel, out_shape=jax.ShapeDtypeStruct((512, W), f32...  105 us
    unnamed x1, local copies, waits for them, and re-layouts  3.16 us

profile of v1, /device:TPU:1, one launch (start us, length us, event | category | flops | bytes accessed | tf_op | source)
XLA Modules:
  0.0 108.3 jit_solution(11198318480486695669)
XLA Ops:
  0.0 105.1 %whole.1 = f32[512,1024]{1,0:T(8,128)} custom-call(f32[512,512]{1,0:T(8,128)} %past_ref.1, f32[512,1024]{1,0:T(8,128)} %a_ref.1), custom_call_target="tpu_custom_call" | custom-call | tf_op jit(solution)/shard_map/whole/pallas_call | solution.py:374
  105.1 3.2 %copy.4 = f32[512,1024]{1,0:T(8,128)} copy(f32[512,1024]{1,0:T(8,128)} %whole.1) | data formatting | bytes 4194304

commit v2 on v1

v2 whole, which is shorter than its diff:
```python
import functools

import jax
import jax.numpy as jnp
from jax import lax
from jax.experimental import pallas as pl
from jax.experimental.pallas import tpu as pltpu
from jax.sharding import Mesh
from jax.sharding import PartitionSpec as P

W = 1024
B = 128
NBLK = W // B
PANEL = 16
AXES = ("row", "col_0", "col_1", "depth")
ROW_COL = ("row", "col_0", "col_1")
NT = (((1,), (1,)), ((), ()))
NN = (((1,), (0,)), ((), ()))
f32 = jnp.float32
bf16 = jnp.bfloat16
MESH = pl.DeviceIdType.MESH
VMEM = pl.BlockSpec(memory_space=pltpu.VMEM)


TILES = (
    (((0, 0), (1, 0), (2, 0), (3, 0)), ((4, 0), (5, 0), (6, 0), (7, 0))),
    (
        ((1, 1), (2, 1), (3, 1), (2, 2), (3, 2), (3, 3)),
        ((4, 1), (5, 1), (6, 1), (7, 1), (4, 2), (5, 2)),
    ),
    (
        ((6, 2), (7, 2), (4, 3), (5, 3), (6, 3), (7, 3), (4, 4), (5, 4)),
        ((6, 4), (7, 4), (5, 5), (6, 5), (7, 5), (6, 6), (7, 6), (7, 7)),
    ),
)
ROWS = (8, 8, 16, 24, 32)
BASE = (0, 256, 0, 1024, 2560)
STRIDE = (512, 512, 512, 768, 1024)
SOURCE = (0, 256, 0, 512, 1280)
SLOT = (0, 0, 0, 16, 40)


def split(x):
    high = x.astype(bf16)
    return high, (x - high.astype(f32)).astype(bf16)


def dot3(a, b, dims=NT):
    dot = functools.partial(
        lax.dot_general, dimension_numbers=dims, preferred_element_type=f32
    )
    return dot(a[0], b[0]) + (dot(a[0], b[1]) + dot(a[1], b[0]))


def top_tiles(part, core, first, th_ref, tl_ref, a_ref, other_a_ref, tiles_ref):
    out = SOURCE[2 + part]

    def blocks(i, n=1):
        return slice(i * B, (i + n) * B)

    def value(i, j):
        if core == 1:
            return a_ref[blocks(i - 4), blocks(j)]
        if i < 4:
            return a_ref[blocks(i), blocks(j)]
        if j < 4:
            return a_ref[blocks(j), blocks(i)].T
        return other_a_ref[blocks(i - 4), blocks(j - 4)]

    todo = list(TILES[part][core])
    while todo:
        i, j = todo[0]
        n = 1
        while n < len(todo) and todo[n] == (i + n, j):
            n += 1
        todo = todo[n:]
        product = dot3(
            (th_ref[blocks(i, n), :], tl_ref[blocks(i, n), :]),
            (th_ref[blocks(j), :], tl_ref[blocks(j), :]),
        )
        for k in range(n):
            tiles_ref[out : out + B, :] = jnp.where(first, value(i + k, j), 0.0) - product[blocks(k)]
            out += B


def whole_kernel(
    past_ref, a_ref, out_ref,
    so_ref, u_ref, top_ref, lh_ref, ll_ref, dh_ref, dl_ref, xh_ref, xl_ref,
    to_ref, other_ref, other_a_ref, tiles_ref, ybuf, th_ref, tl_ref, part_ref, half_ref, full_ref,
    sc_send, sc_recv, y_send, y_recv, z_send, z_recv, x_send, x_recv, d_send, d_recv,
    r_send, r_recv, g_send, g_recv, loc, swap,
):
    x = lax.axis_index("row")
    z = lax.axis_index("col_0")
    c = lax.axis_index("col_1")
    y = lax.axis_index("depth")
    me = x * 8 + z
    left = lax.rem(x + 3, 4)
    right = lax.rem(x + 1, 4)
    far = lax.rem(x + 2, 4)
    down = lax.rem(y + 3, 4)
    up = lax.rem(y + 1, 4)
    root = me == 0
    barrier = pltpu.get_barrier_semaphore()

    def greet(*device):
        pl.semaphore_signal(barrier, inc=1, device_id=device, device_id_type=MESH)

    def z_greet(k, carry):
        greet(x, lax.rem(z + k, 8), c, y)
        return carry

    lax.fori_loop(1, 8, z_greet, 0)
    for k in range(1, 4):
        greet(x, z, c, lax.rem(y + k, 4))
    greet(left, z, c, y)
    greet(right, z, c, y)
    greet(x, z, 1 - c, y)

    @pl.when(jnp.logical_not(root))
    def _():
        greet(0, 0, c, y)
        pl.semaphore_wait(barrier, 13)

    @pl.when(root)
    def _():
        pl.semaphore_wait(barrier, 44)

    def remote(src, dst, send, recv, *device):
        return pltpu.make_async_remote_copy(
            src_ref=src, dst_ref=dst, send_sem=send, recv_sem=recv,
            device_id=device, device_id_type=MESH,
        )


    def pieces(n, core, start, count):
        at = pl.multiple_of(BASE[n] + core * STRIDE[n] + start * ROWS[n], 8)
        return (to_ref if n < 2 else so_ref).at[pl.ds(at, count * ROWS[n])]

    def slot(n, layer):
        return ybuf.at[layer, pl.ds(SLOT[n], ROWS[n])]

    def source(n, q):
        at = pl.multiple_of(SOURCE[n] + q * ROWS[n], 8)
        return (past_ref if n < 2 else tiles_ref).at[pl.ds(at, ROWS[n])]

    def scatter(n, q):
        dst = pieces(n, c, q, 1) if n < 2 else slot(n, y)
        return remote(source(n, q), dst, sc_send.at[n, q], sc_recv.at[n], q // 8, lax.rem(q, 8), c, y)

    def own(n):
        dst = pieces(n, c, 0, 1) if n < 2 else slot(n, y)
        return pltpu.make_async_copy(source(n, 0), dst, loc.at[n])

    def scatter_all(n):
        own(n).start()

        def go(q, carry):
            scatter(n, q).start()
            return carry

        lax.fori_loop(1, 32, go, 0)
        own(n).wait()

    def scatter_wait(n):
        @pl.when(jnp.logical_not(root))
        def _():
            dst = pieces(n, c, me, 1) if n < 2 else slot(n, y)
            remote(source(n, 0), dst, sc_send.at[n, 0], sc_recv.at[n], 0, 0, c, y).wait_recv()

    def y_copy(n, k):
        return remote(slot(n, y), slot(n, y), y_send.at[n, k], y_recv.at[n, y], x, z, c, lax.rem(y + k, 4))

    def z_copy(n, k):
        mine = pieces(n, c, me, 1)
        return remote(mine, mine, z_send.at[n, k], z_recv.at[n, z], x, lax.rem(z + k, 8), c, y)

    def z_start(n):
        def go(k, carry):
            z_copy(n, k).start()
            return carry

        lax.fori_loop(1, 8, go, 0)

    def z_wait(n):
        def wait(k, carry):
            peer = lax.rem(z + k, 8)
            place = pieces(n, c, x * 8 + peer, 1)
            remote(place, place, z_send.at[n, 0], z_recv.at[n, peer], x, peer, c, y).wait_recv()
            return carry

        lax.fori_loop(1, 8, wait, 0)

    def group(n, core, g):
        return pieces(n, core, g * 8, 8)

    def half(n, g, h):
        return pieces(n, c, g * 8 + h * 4, 4)

    def x_copy(n, d):
        mine = group(n, c, x)
        return remote(mine, mine, x_send.at[n, d], x_recv.at[n, d], (right, left)[d], z, c, y)

    def x_wait(n, d):
        g = (left, right)[d]
        place = group(n, c, g)
        remote(place, place, x_send.at[n, d], x_recv.at[n, d], g, z, c, y).wait_recv()

    def relay(n, d):
        part = half(n, (left, right)[d], d)
        return remote(part, part, x_send.at[n, 2 + d], x_recv.at[n, 2 + d], (right, left)[d], z, c, y)

    def relay_wait(n, d):
        place = half(n, far, d)
        remote(place, place, x_send.at[n, 2 + d], x_recv.at[n, 2 + d], (left, right)[d], z, c, y).wait_recv()

    order = (x, left, right, far)

    def cross(n, k):
        place = group(n, c, order[k])
        return remote(place, place, d_send.at[n, k], d_recv.at[n, k], x, z, 1 - c, y)

    def stage_1(n):
        scatter_wait(n)
        if n < 2:
            z_start(n)
        else:
            for k in range(1, 4):
                y_copy(n, k).start()

    def stage_y(n):
        for k in range(1, 4):
            peer = lax.rem(y + k, 4)
            place = slot(n, peer)
            remote(place, place, y_send.at[n, 0], y_recv.at[n, peer], x, z, c, peer).wait_recv()
        rows = slice(SLOT[n], SLOT[n] + ROWS[n])
        at = pl.multiple_of(BASE[n] + c * STRIDE[n] + me * ROWS[n], 8)
        so_ref[pl.ds(at, ROWS[n]), :] = (ybuf[0, rows] + ybuf[1, rows]) + (ybuf[2, rows] + ybuf[3, rows])
        z_start(n)

    def stage_2(n):
        z_wait(n)
        for d in range(2):
            x_copy(n, d).start()
        cross(n, 0).start()

    def stage_3(n):
        for d in range(2):
            x_wait(n, d)
            relay(n, d).start()
            cross(n, 1 + d).start()

    def stage_4(n):
        for d in range(2):
            relay_wait(n, d)
        cross(n, 3).start()

    def stage_5(n):
        for k in range(4):
            place = group(n, 1 - c, order[k])
            remote(place, place, d_send.at[n, k], d_recv.at[n, k], x, z, 1 - c, y).wait_recv()


    def update(h):
        for n in range(2):
            at = slice(n * 512 + h * 256, n * 512 + h * 256 + 256)
            th_ref[at, :], tl_ref[at, :] = split(to_ref[at, :])
        for k in (2, 1, 3, 0):
            at = pl.multiple_of(lax.rem(y + k, 4) * B, B)
            mine = split(past_ref[pl.ds(at, B), :])
            for n in range(2):
                top = slice(n * 512 + h * 256, n * 512 + h * 256 + 256)
                part_ref[k, h, :, n * 256 : n * 256 + 256] = dot3(mine, (th_ref[top, :], tl_ref[top, :]))
            if k == 2:
                for d in range(2):
                    reduce_first(h, d).start()
            elif k:
                reduce_own(h, k // 2).start()

    def reduce_first(h, d):
        return remote(
            part_ref.at[2, h, pl.ds(d * 64, 64)], half_ref.at[h, d], r_send.at[h, d], r_recv.at[h, d],
            x, z, c, (up, down)[d],
        )

    def reduce_own(h, d):
        rows = pl.ds(64 - d * 64, 64)
        return remote(
            part_ref.at[1 + 2 * d, h, rows], full_ref.at[h, d, rows], r_send.at[h, 2 + d], r_recv.at[h, 2 + d],
            x, z, c, (up, down)[d],
        )

    def reduce_sum(h, d):
        rows = pl.ds(d * 64, 64)
        return remote(
            part_ref.at[1 + 2 * d, h, rows], full_ref.at[h, d, rows], r_send.at[h, 4 + d], r_recv.at[h, 4 + d],
            x, z, c, (up, down)[d],
        )

    def update_2(h):
        for d in range(2):
            reduce_first(h, d).wait_recv()
            rows = slice(d * 64, d * 64 + 64)
            part_ref[1 + 2 * d, h, rows, :] += half_ref[h, d]
            reduce_sum(h, d).start()

    def gather(h, d):
        to = pl.ds((1 + 2 * d) * B, B)
        return remote(
            u_ref.at[h, pl.ds(0, B)], u_ref.at[h, to], g_send.at[h, d], g_recv.at[h, d], x, z, c, (up, down)[d]
        )

    def gather_on(h, d):
        mine = pl.ds((1 + 2 * d) * B + d * 64, 64)
        to = pl.ds(2 * B + d * 64, 64)
        return remote(
            u_ref.at[h, mine], u_ref.at[h, to], g_send.at[h, 2 + d], g_recv.at[h, 2 + d], x, z, c, (up, down)[d]
        )

    def update_3(h):
        for d in range(2):
            reduce_own(h, d).wait_recv()
            reduce_sum(h, d).wait_recv()
        at = pl.multiple_of(y * B, B)
        for n in range(2):
            cols = slice(n * 256, n * 256 + 256)
            mat = a_ref[pl.ds(at, B), n * 512 + h * 256 : n * 512 + h * 256 + 256]
            u_ref[h, 0:B, cols] = mat - (part_ref[0, h, :, cols] + (full_ref[h, 0, :, cols] + full_ref[h, 1, :, cols]))
        for d in range(2):
            gather(h, d).start()

    def update_4(h):
        for d in range(2):
            gather(h, d).wait_recv()
            gather_on(h, d).start()

    def update_5(h):
        for d in range(2):
            gather_on(h, d).wait_recv()

    def take(part):
        for core in range(2):
            at = BASE[2 + part] + core * STRIDE[2 + part]
            for n, (i, j) in enumerate(TILES[part][core]):
                top_ref[i * B : i * B + B, j * B : j * B + B] += so_ref[at + n * B : at + n * B + B, :]


    trade = remote(past_ref, other_ref, swap.at[0], swap.at[1], x, z, 1 - c, y)
    trade_a = remote(a_ref.at[:, pl.ds(512, 512)], other_a_ref, swap.at[2], swap.at[3], x, z, 1 - c, y)

    @pl.when(root)
    def _():
        trade.start()
        trade_a.start()
        scatter_all(0)
        z_start(0)
        scatter_all(1)
        z_start(1)
        mine = pl.ds(pl.multiple_of(c * 512, 512), 512)
        theirs = pl.ds(pl.multiple_of(512 - c * 512, 512), 512)
        th_ref[mine, :], tl_ref[mine, :] = split(past_ref[...])
        trade.wait_recv()
        th_ref[theirs, :], tl_ref[theirs, :] = split(other_ref[...])
        trade_a.wait_recv()
        for part in range(3):
            for core in range(2):
                @pl.when(c == core)
                def _(part=part, core=core):
                    top_tiles(part, core, y == 0, th_ref, tl_ref, a_ref, other_a_ref, tiles_ref)

            scatter_all(2 + part)

    @pl.when(jnp.logical_not(root))
    def _():
        for i in range(NBLK):
            top_ref[i * B : i * B + B, 0 : i * B + B] = jnp.zeros((B, i * B + B), f32)
        stage_1(0)
        stage_1(1)

    @pl.when(root)
    def _():
        for i in range(NBLK):
            top_ref[i * B : i * B + B, 0 : i * B + B] = jnp.zeros((B, i * B + B), f32)

    rows_0, rows_1, tiles_a, tiles_b, tiles_c = range(5)
    stage_2(rows_0)
    stage_1(tiles_a)
    stage_2(rows_1)
    stage_y(tiles_a)
    stage_3(rows_0)
    stage_1(tiles_b)
    stage_4(rows_0)
    stage_y(tiles_b)
    stage_2(tiles_a)
    stage_3(rows_1)
    stage_5(rows_0)
    update(0)
    stage_1(tiles_c)
    stage_3(tiles_a)
    stage_4(rows_1)
    stage_2(tiles_b)
    stage_y(tiles_c)
    stage_4(tiles_a)
    stage_5(rows_1)
    update(1)
    stage_5(tiles_a)
    take(0)

    def stage_5b():
        stage_5(tiles_b)
        take(1)

    def stage_5c():
        stage_5(tiles_c)
        take(2)

    events = {
        (0, 1): (lambda: update_2(0),),
        (0, 3): (lambda: stage_3(tiles_b),),
        (0, 7): (lambda: stage_4(tiles_b),),
        (1, -1): (stage_5b,),
        (1, 2): (lambda: stage_2(tiles_c),),
        (1, 4): (lambda: update_2(1),),
        (2, 1): (lambda: stage_3(tiles_c),),
        (2, 5): (lambda: update_3(0),),
        (2, 7): (lambda: stage_4(tiles_c),),
        (3, 0): (stage_5c,),
        (4, 3): (lambda: update_3(1),),
        (4, 6): (lambda: update_4(0),),
        (6, 4): (lambda: update_4(1),),
    }
    factor_top(lh_ref, ll_ref, dh_ref, dl_ref, top_ref, events)
    update_5(0)
    update_5(1)
    solve(y, (x * 16 + z * 2 + c) * 512, u_ref, lh_ref, ll_ref, dh_ref, dl_ref, out_ref, xh_ref, xl_ref)


    @pl.when(root)
    def _():
        trade.wait_send()
        trade_a.wait_send()

        def done(q, carry):
            for n in range(5):
                scatter(n, q).wait_send()
            return carry

        lax.fori_loop(1, 32, done, 0)

    def done_z(k, carry):
        for n in range(5):
            z_copy(n, k).wait_send()
        return carry

    lax.fori_loop(1, 8, done_z, 0)
    for n in range(5):
        if n >= 2:
            for k in range(1, 4):
                y_copy(n, k).wait_send()
        for d in range(2):
            x_copy(n, d).wait_send()
            relay(n, d).wait_send()
        for k in range(4):
            cross(n, k).wait_send()
    for h in range(2):
        for d in range(2):
            reduce_first(h, d).wait_send()
            reduce_own(h, d).wait_send()
            reduce_sum(h, d).wait_send()
            gather(h, d).wait_send()
            gather_on(h, d).wait_send()


def inverse_factor(w, fill):
    lane = lax.broadcasted_iota(jnp.int32, (B, B), 1)
    sub = lax.broadcasted_iota(jnp.int32, (B, B), 0)
    k = PANEL
    at = sub[:k]
    done = []
    for t in range(B // k):
        r0 = t * k
        left = B - r0
        cols = [jnp.broadcast_to(w[:, r0 + m : r0 + m + 1], (left, B)) for m in range(k)]
        lanes, subs = lane[:left], sub[:left]
        unit = jnp.where((lanes == subs + r0) & (subs < k), 1.0, 0.0)
        w = jnp.where((lanes >= r0) & (lanes < r0 + k), unit, w)
        rows = w[:k]
        piv = jnp.stack([col[:k] for col in cols])
        final = jnp.zeros((k, B), f32)
        for m in range(k):
            mine, rest = piv[0], piv[1:]
            inv = lax.rsqrt(jnp.broadcast_to(mine[m : m + 1], (k, B)))
            inv2 = inv * inv
            row = jnp.broadcast_to(rows[m : m + 1], (k, B))
            here = at == m
            final = jnp.where(here, row * inv, final)
            step = row * inv2
            rows = jnp.where(here, step, rows - mine * step)
            if m + 1 < k:
                f = jnp.broadcast_to(rest[:, m : m + 1], (k - 1 - m, k, B)) * inv2[None]
                piv = jnp.where(here[None], f, rest - mine[None] * f)
        done.append(jnp.where(lane[:k] <= at + r0, final, 0.0))
        if left > k:
            w = w[k:]
            for m in range(k):
                w = w - cols[m][k:] * jnp.broadcast_to(rows[m : m + 1], (left - k, B))
        fill(t)
    return jnp.concatenate(done, axis=0)


def factor_top(lh_ref, ll_ref, dh_ref, dl_ref, a_ref, events):
    def rows(i, n=1):
        return slice(i * B, (i + n) * B)

    def low(i, n, j):
        return lh_ref[rows(i, n), rows(j)], ll_ref[rows(i, n), rows(j)]

    def panel(i, n, s, d):
        high, lo = split(dot3(split(a_ref[rows(i, n), rows(s)]), d))
        lh_ref[rows(i, n), rows(s)] = high
        ll_ref[rows(i, n), rows(s)] = lo

    def trail(i, n, j, nj, s):
        a_ref[rows(i, n), rows(j, nj)] -= dot3(low(i, n, s), low(j, nj, s))

    waiting = []
    halves = [None, None]
    for s in range(NBLK):
        def fill(t, s=s):
            for event in events.get((s, t), ()):
                event()
            n = -(-len(waiting) // (B // PANEL - t))
            for _ in range(n):
                waiting.pop(0)()

        for event in events.get((s, -1), ()):
            event()
        d = split(inverse_factor(a_ref[rows(s), rows(s)], fill))
        halves[s % 2] = d
        at = (s % 2) * B
        dh_ref[s // 2, at : at + B, at : at + B] = d[0]
        dl_ref[s // 2, at : at + B, at : at + B] = d[1]
        if s % 2 == 0:
            dh_ref[s // 2, 0:B, B : 2 * B] = jnp.zeros((B, B), bf16)
            dl_ref[s // 2, 0:B, B : 2 * B] = jnp.zeros((B, B), bf16)
        if s + 1 < NBLK:
            panel(s + 1, 1, s, d)
            trail(s + 1, 1, s + 1, 1, s)
        if s + 2 < NBLK:
            def rest(s=s, d=d):
                panel(s + 2, NBLK - s - 2, s, d)

            waiting.append(rest)
            waiting.append(functools.partial(trail, s + 2, NBLK - s - 2, s + 1, 1, s))
            for j in range(s + 2, NBLK):
                waiting.append(functools.partial(trail, j, NBLK - j, j, 1, s))
        if s % 2 == 1:
            def corner(s=s, first=halves[0], second=halves[1]):
                mid = dot3(low(s, 1, s - 1), first, NN)
                high, lo = split(-dot3(second, split(mid), NN))
                dh_ref[s // 2, B : 2 * B, 0:B] = high
                dl_ref[s // 2, B : 2 * B, 0:B] = lo

            waiting.append(corner)
    for job in waiting:
        job()


def solve(depth, base, u_ref, lh_ref, ll_ref, dh_ref, dl_ref, out_ref, xh, xl):
    for n in range(4):
        cols = slice(n * 256, n * 256 + 256)
        u = u_ref[n % 2, :, (n // 2) * 256 : (n // 2) * 256 + 256]
        if n:
            done = slice(0, n * 256)
            u = u - dot3((xh[:, done], xl[:, done]), (lh_ref[cols, done], ll_ref[cols, done]))
        out = dot3(split(u), (dh_ref[n], dl_ref[n]))
        xh[:, cols], xl[:, cols] = split(out)
        col = lax.broadcasted_iota(jnp.int32, (B, 256), 1) + n * 256
        for q in range(4):
            place = pl.multiple_of(lax.rem(depth + 4 - q, 4) * B, B)
            row = lax.broadcasted_iota(jnp.int32, (B, 256), 0) + (base + place)
            out_ref[pl.ds(place, B), cols] = jnp.where(row >= col, out[q * B : q * B + B, :], 0.0)


def body(a_cols, past):
    dma = pltpu.SemaphoreType.DMA
    vmem = pltpu.VMEM
    return pl.pallas_call(
        whole_kernel,
        out_shape=jax.ShapeDtypeStruct((512, W), f32),
        in_specs=[VMEM] * 2,
        out_specs=VMEM,
        scratch_shapes=[
            vmem((36 * B, B), f32),
            vmem((2, 4 * B, 512), f32),
            vmem((W, W), f32),
            vmem((W, W), bf16),
            vmem((W, W), bf16),
            vmem((4, 256, 256), bf16),
            vmem((4, 256, 256), bf16),
            vmem((4 * B, W), bf16),
            vmem((4 * B, W), bf16),
            vmem((W, 512), f32),
            vmem((512, 512), f32),
            vmem((512, 512), f32),
            vmem((18 * B, B), f32),
            vmem((4, 72, B), f32),
            vmem((W, 512), bf16),
            vmem((W, 512), bf16),
            vmem((4, 2, B, 512), f32),
            vmem((2, 2, 64, 512), f32),
            vmem((2, 2, B, 512), f32),
            dma((5, 32)), dma((5,)), dma((5, 4)), dma((5, 4)), dma((5, 8)), dma((5, 8)),
            dma((5, 4)), dma((5, 4)), dma((5, 4)), dma((5, 4)),
            dma((2, 6)), dma((2, 6)), dma((2, 4)), dma((2, 4)), dma((5,)), dma((4,)),
        ],
        compiler_params=pltpu.CompilerParams(collective_id=0, has_side_effects=True),
        name="whole",
    )(past, a_cols)


def solution(mesh):
    split_mesh = Mesh(
        mesh.devices.reshape(mesh.shape["row"], 8, 2, mesh.shape["depth"]), AXES
    )
    placed = (P(ROW_COL, None), P(ROW_COL, "depth"))
    return jax.shard_map(
        body, mesh=split_mesh, in_specs=placed, out_specs=P(ROW_COL, None), check_vma=False
    )
```

time: 109 us -> 108 us (level)
  no operation moved by 1% of the time
where the time goes in v2:
time: 108 us; the launch traced here: 107 us
  Pallas kernels  104 us (96%)
  local copies, waits for them, and re-layouts  3.16 us (3%)
    pallas_call x1, Pallas kernels, body(): pl.pallas_call(whole_kernel, out_shape=jax.ShapeDtypeStruct((512, W), f32...  104 us
    unnamed x1, local copies, waits for them, and re-layouts  3.16 us

profile of v2, /device:TPU:1, one launch (start us, length us, event | category | flops | bytes accessed | tf_op | source)
XLA Modules:
  0.0 107.5 jit_solution(10616038186386364389)
XLA Ops:
  0.0 104.3 %whole.1 = f32[512,1024]{1,0:T(8,128)} custom-call(f32[512,512]{1,0:T(8,128)} %past_ref.1, f32[512,1024]{1,0:T(8,128)} %a_ref.1), custom_call_target="tpu_custom_call" | custom-call | tf_op jit(solution)/shard_map/whole/pallas_call | solution.py:588
  104.3 3.2 %copy.4 = f32[512,1024]{1,0:T(8,128)} copy(f32[512,1024]{1,0:T(8,128)} %whole.1) | data formatting | bytes 4194304

commit v3 on v2

--- a/solution.py
+++ b/solution.py
@@ -84,10 +84,10 @@
 
 
 def whole_kernel(
-    past_ref, a_ref, out_ref,
-    so_ref, u_ref, top_ref, lh_ref, ll_ref, dh_ref, dl_ref, xh_ref, xl_ref,
-    to_ref, other_ref, other_a_ref, tiles_ref, ybuf, th_ref, tl_ref, part_ref, half_ref, full_ref,
-    sc_send, sc_recv, y_send, y_recv, z_send, z_recv, x_send, x_recv, d_send, d_recv,
+    past_in, a_in, out_ref,
+    past_ref, a_ref, perm_ref, so_ref, u_ref, top_ref, lh_ref, ll_ref, dh_ref, dl_ref, xh_ref, xl_ref,
+    to_ref, other_ref, other_a_ref, tiles_ref, ybuf, th_ref, tl_ref, part_ref, half_ref, full_ref, bun_t, bun_s,
+    sc_send, sc_recv, bu_recv, fw_send, y_send, y_recv, z_send, z_recv, x_send, x_recv, d_send, d_recv,
     r_send, r_recv, g_send, g_recv, loc, swap,
 ):
     x = lax.axis_index("row")
@@ -101,6 +101,12 @@
     down = lax.rem(y + 3, 4)
     up = lax.rem(y + 1, 4)
     root = me == 0
+    load = (
+        pltpu.make_async_copy(past_in, past_ref, loc.at[5]),
+        pltpu.make_async_copy(a_in, a_ref, loc.at[6]),
+    )
+    for copy in load:
+        copy.start()
     barrier = pltpu.get_barrier_semaphore()
 
     def greet(*device):
@@ -113,18 +119,17 @@
     lax.fori_loop(1, 8, z_greet, 0)
     for k in range(1, 4):
         greet(x, z, c, lax.rem(y + k, 4))
-    greet(left, z, c, y)
-    greet(right, z, c, y)
+    for k in range(1, 4):
+        greet(lax.rem(x + k, 4), z, c, y)
     greet(x, z, 1 - c, y)
 
-    @pl.when(jnp.logical_not(root))
-    def _():
-        greet(0, 0, c, y)
-        pl.semaphore_wait(barrier, 13)
-
-    @pl.when(root)
-    def _():
-        pl.semaphore_wait(barrier, 44)
+    for copy in load:
+        copy.wait()
+    for h in range(2):
+        for q in range(32):
+            to = (h * 32 + q % 8 * 4 + q // 8) * 8
+            perm_ref[to : to + 8, :] = past_ref[(h * 32 + q) * 8 : (h * 32 + q) * 8 + 8, :]
+    pl.semaphore_wait(barrier, 14)
 
     def remote(src, dst, send, recv, *device):
         return pltpu.make_async_remote_copy(
@@ -140,33 +145,58 @@
     def slot(n, layer):
         return ybuf.at[layer, pl.ds(SLOT[n], ROWS[n])]
 
-    def source(n, q):
-        at = pl.multiple_of(SOURCE[n] + q * ROWS[n], 8)
-        return (past_ref if n < 2 else tiles_ref).at[pl.ds(at, ROWS[n])]
-
-    def scatter(n, q):
-        dst = pieces(n, c, q, 1) if n < 2 else slot(n, y)
-        return remote(source(n, q), dst, sc_send.at[n, q], sc_recv.at[n], q // 8, lax.rem(q, 8), c, y)
-
-    def own(n):
-        dst = pieces(n, c, 0, 1) if n < 2 else slot(n, y)
-        return pltpu.make_async_copy(source(n, 0), dst, loc.at[n])
-
-    def scatter_all(n):
-        own(n).start()
-
-        def go(q, carry):
-            scatter(n, q).start()
+
+    def source(n, start, count):
+        at = pl.multiple_of(SOURCE[n] + start * ROWS[n], 8)
+        return (perm_ref if n < 2 else tiles_ref).at[pl.ds(at, count * ROWS[n])]
+
+    def width(n):
+        return 4 if n < 2 else 8
+
+    def place_of(n, q):
+        return pieces(n, c, q, 1) if n < 2 else slot(n, y)
+
+    def bundle(n, start, count):
+        ref, at = (bun_t, n * 32) if n < 2 else (bun_s, 8 * SLOT[n])
+        return ref.at[pl.ds(at + start * ROWS[n], count * ROWS[n])]
+
+    def column(n, to):
+        place = (0, to) if n < 2 else (to, 0)
+        src = source(n, to * width(n), width(n))
+        return remote(src, bundle(n, 0, width(n)), sc_send.at[n, to], bu_recv.at[n], *place, c, y)
+
+    def columns_all(n):
+        def go(to, carry):
+            column(n, to).start()
             return carry
 
-        lax.fori_loop(1, 32, go, 0)
-        own(n).wait()
-
-    def scatter_wait(n):
-        @pl.when(jnp.logical_not(root))
+        lax.fori_loop(1, 8 if n < 2 else 4, go, 0)
+
+    def first_piece(n, on_root, k):
+        return source(n, k, 1) if on_root else bundle(n, k, 1)
+
+    def onward(n, on_root, k):
+        place = (k, z) if n < 2 else (x, k)
+        dst = place_of(n, place[0] * 8 + place[1])
+        return remote(first_piece(n, on_root, k), dst, fw_send.at[n, k], sc_recv.at[n], *place, c, y)
+
+    def hub(n):
+        return jnp.logical_and(x == 0 if n < 2 else z == 0, jnp.logical_not(root))
+
+    def pass_on(n, on_root):
+        own = pltpu.make_async_copy(first_piece(n, on_root, 0), place_of(n, me), loc.at[n])
+        own.start()
+        for k in range(1, width(n)):
+            onward(n, on_root, k).start()
+        own.wait()
+
+    def stage_h(n):
+        @pl.when(hub(n))
         def _():
-            dst = pieces(n, c, me, 1) if n < 2 else slot(n, y)
-            remote(source(n, 0), dst, sc_send.at[n, 0], sc_recv.at[n], 0, 0, c, y).wait_recv()
+            whole = bundle(n, 0, width(n))
+            remote(whole, whole, sc_send.at[n, 0], bu_recv.at[n], 0, 0, c, y).wait_recv()
+            pass_on(n, False)
+            send_piece(n)
 
     def y_copy(n, k):
         return remote(slot(n, y), slot(n, y), y_send.at[n, k], y_recv.at[n, y], x, z, c, lax.rem(y + k, 4))
@@ -220,13 +250,24 @@
         place = group(n, c, order[k])
         return remote(place, place, d_send.at[n, k], d_recv.at[n, k], x, z, 1 - c, y)
 
-    def stage_1(n):
-        scatter_wait(n)
+    def send_piece(n):
         if n < 2:
             z_start(n)
         else:
             for k in range(1, 4):
                 y_copy(n, k).start()
+
+    def stage_0(n):
+        columns_all(n)
+        pass_on(n, True)
+        send_piece(n)
+
+    def stage_1(n):
+        @pl.when(x != 0 if n < 2 else z != 0)
+        def _():
+            place = place_of(n, me)
+            remote(place, place, sc_send.at[n, 0], sc_recv.at[n], 0, z, c, y).wait_recv()
+            send_piece(n)
 
     def stage_y(n):
         for k in range(1, 4):
@@ -240,15 +281,15 @@
 
     def stage_2(n):
         z_wait(n)
+        cross(n, 0).start()
         for d in range(2):
             x_copy(n, d).start()
-        cross(n, 0).start()
 
     def stage_3(n):
         for d in range(2):
             x_wait(n, d)
+            cross(n, 1 + d).start()
             relay(n, d).start()
-            cross(n, 1 + d).start()
 
     def stage_4(n):
         for d in range(2):
@@ -352,10 +393,8 @@
     def _():
         trade.start()
         trade_a.start()
-        scatter_all(0)
-        z_start(0)
-        scatter_all(1)
-        z_start(1)
+        stage_0(0)
+        stage_0(1)
         mine = pl.ds(pl.multiple_of(c * 512, 512), 512)
         theirs = pl.ds(pl.multiple_of(512 - c * 512, 512), 512)
         th_ref[mine, :], tl_ref[mine, :] = split(past_ref[...])
@@ -368,40 +407,51 @@
                 def _(part=part, core=core):
                     top_tiles(part, core, y == 0, th_ref, tl_ref, a_ref, other_a_ref, tiles_ref)
 
-            scatter_all(2 + part)
-
-    @pl.when(jnp.logical_not(root))
-    def _():
-        for i in range(NBLK):
-            top_ref[i * B : i * B + B, 0 : i * B + B] = jnp.zeros((B, i * B + B), f32)
-        stage_1(0)
-        stage_1(1)
-
-    @pl.when(root)
-    def _():
-        for i in range(NBLK):
-            top_ref[i * B : i * B + B, 0 : i * B + B] = jnp.zeros((B, i * B + B), f32)
+        stage_0(2)
 
     rows_0, rows_1, tiles_a, tiles_b, tiles_c = range(5)
+
+    for i in range(NBLK):
+        top_ref[i * B : i * B + B, 0 : i * B + B] = jnp.zeros((B, i * B + B), f32)
+
+    def next_part(n):
+        @pl.when(root)
+        def _():
+            stage_0(n)
+
+    def next_part(n):
+        @pl.when(root)
+        def _():
+            stage_0(n)
+
+    stage_h(rows_0)
+    stage_1(rows_0)
+    stage_h(tiles_a)
+    stage_h(rows_1)
     stage_2(rows_0)
+    next_part(tiles_b)
+    stage_1(rows_1)
     stage_1(tiles_a)
+    stage_3(rows_0)
+    stage_y(tiles_a)
+    stage_4(rows_0)
+    stage_h(tiles_b)
     stage_2(rows_1)
-    stage_y(tiles_a)
-    stage_3(rows_0)
-    stage_1(tiles_b)
-    stage_4(rows_0)
-    stage_y(tiles_b)
-    stage_2(tiles_a)
-    stage_3(rows_1)
+    next_part(tiles_c)
     stage_5(rows_0)
     update(0)
+    stage_2(tiles_a)
+    stage_1(tiles_b)
+    stage_3(rows_1)
+    stage_3(tiles_a)
+    stage_y(tiles_b)
+    stage_h(tiles_c)
+    stage_4(rows_1)
+    stage_4(tiles_a)
+    update_2(0)
+    stage_5(rows_1)
+    stage_2(tiles_b)
     stage_1(tiles_c)
-    stage_3(tiles_a)
-    stage_4(rows_1)
-    stage_2(tiles_b)
-    stage_y(tiles_c)
-    stage_4(tiles_a)
-    stage_5(rows_1)
     update(1)
     stage_5(tiles_a)
     take(0)
@@ -414,25 +464,35 @@
         stage_5(tiles_c)
         take(2)
 
+    finish = functools.partial(
+        solve, y, u_ref, lh_ref, ll_ref, dh_ref, dl_ref, out_ref, xh_ref, xl_ref
+    )
+
+    def update_5ab():
+        update_5(0)
+        update_5(1)
+
     events = {
-        (0, 1): (lambda: update_2(0),),
-        (0, 3): (lambda: stage_3(tiles_b),),
-        (0, 7): (lambda: stage_4(tiles_b),),
-        (1, -1): (stage_5b,),
-        (1, 2): (lambda: stage_2(tiles_c),),
-        (1, 4): (lambda: update_2(1),),
-        (2, 1): (lambda: stage_3(tiles_c),),
-        (2, 5): (lambda: update_3(0),),
-        (2, 7): (lambda: stage_4(tiles_c),),
-        (3, 0): (stage_5c,),
-        (4, 3): (lambda: update_3(1),),
-        (4, 6): (lambda: update_4(0),),
-        (6, 4): (lambda: update_4(1),),
+        (0, 0): lambda: stage_3(tiles_b),
+        (0, 1): lambda: stage_y(tiles_c),
+        (0, 4): lambda: stage_4(tiles_b),
+        (0, 6): lambda: update_2(1),
+        (1, -1): stage_5b,
+        (1, 1): lambda: stage_2(tiles_c),
+        (1, 3): lambda: update_3(0),
+        (1, 7): lambda: stage_3(tiles_c),
+        (2, 4): lambda: update_3(1),
+        (2, 7): lambda: stage_4(tiles_c),
+        (3, 0): stage_5c,
+        (3, 6): lambda: update_4(0),
+        (5, 1): lambda: update_4(1),
+        (6, 5): update_5ab,
+        (7, 0): lambda: finish(0),
+        (7, 2): lambda: finish(1),
+        (7, 4): lambda: finish(2),
     }
     factor_top(lh_ref, ll_ref, dh_ref, dl_ref, top_ref, events)
-    update_5(0)
-    update_5(1)
-    solve(y, (x * 16 + z * 2 + c) * 512, u_ref, lh_ref, ll_ref, dh_ref, dl_ref, out_ref, xh_ref, xl_ref)
+    finish(3)
 
 
     @pl.when(root)
@@ -440,12 +500,17 @@
         trade.wait_send()
         trade_a.wait_send()
 
-        def done(q, carry):
-            for n in range(5):
-                scatter(n, q).wait_send()
-            return carry
-
-        lax.fori_loop(1, 32, done, 0)
+        for n in range(5):
+            for to in range(1, 8 if n < 2 else 4):
+                column(n, to).wait_send()
+            for k in range(1, width(n)):
+                onward(n, True, k).wait_send()
+
+    for n in range(5):
+        @pl.when(hub(n))
+        def _(n=n):
+            for k in range(1, width(n)):
+                onward(n, False, k).wait_send()
 
     def done_z(k, carry):
         for n in range(5):
@@ -527,14 +592,14 @@
     halves = [None, None]
     for s in range(NBLK):
         def fill(t, s=s):
-            for event in events.get((s, t), ()):
-                event()
+            if (s, t) in events:
+                events[s, t]()
             n = -(-len(waiting) // (B // PANEL - t))
             for _ in range(n):
                 waiting.pop(0)()
 
-        for event in events.get((s, -1), ()):
-            event()
+        if (s, -1) in events:
+            events[s, -1]()
         d = split(inverse_factor(a_ref[rows(s), rows(s)], fill))
         halves[s % 2] = d
         at = (s % 2) * B
@@ -566,31 +631,32 @@
         job()
 
 
-def solve(depth, base, u_ref, lh_ref, ll_ref, dh_ref, dl_ref, out_ref, xh, xl):
-    for n in range(4):
-        cols = slice(n * 256, n * 256 + 256)
-        u = u_ref[n % 2, :, (n // 2) * 256 : (n // 2) * 256 + 256]
-        if n:
-            done = slice(0, n * 256)
-            u = u - dot3((xh[:, done], xl[:, done]), (lh_ref[cols, done], ll_ref[cols, done]))
-        out = dot3(split(u), (dh_ref[n], dl_ref[n]))
+def solve(depth, u_ref, lh_ref, ll_ref, dh_ref, dl_ref, out_ref, xh, xl, n):
+    cols = slice(n * 256, n * 256 + 256)
+    u = u_ref[n % 2, :, (n // 2) * 256 : (n // 2) * 256 + 256]
+    if n:
+        done = slice(0, n * 256)
+        u = u - dot3((xh[:, done], xl[:, done]), (lh_ref[cols, done], ll_ref[cols, done]))
+    out = dot3(split(u), (dh_ref[n], dl_ref[n]))
+    if n < 3:
         xh[:, cols], xl[:, cols] = split(out)
-        col = lax.broadcasted_iota(jnp.int32, (B, 256), 1) + n * 256
-        for q in range(4):
-            place = pl.multiple_of(lax.rem(depth + 4 - q, 4) * B, B)
-            row = lax.broadcasted_iota(jnp.int32, (B, 256), 0) + (base + place)
-            out_ref[pl.ds(place, B), cols] = jnp.where(row >= col, out[q * B : q * B + B, :], 0.0)
+    for q in range(4):
+        place = pl.multiple_of(lax.rem(depth + 4 - q, 4) * B, B)
+        out_ref[pl.ds(place, B), cols] = out[q * B : q * B + B, :]
 
 
 def body(a_cols, past):
     dma = pltpu.SemaphoreType.DMA
     vmem = pltpu.VMEM
-    return pl.pallas_call(
+    solved = pl.pallas_call(
         whole_kernel,
         out_shape=jax.ShapeDtypeStruct((512, W), f32),
-        in_specs=[VMEM] * 2,
+        in_specs=[pl.BlockSpec(memory_space=pltpu.HBM)] * 2,
         out_specs=VMEM,
         scratch_shapes=[
+            vmem((512, 512), f32),
+            vmem((512, W), f32),
+            vmem((512, 512), f32),
             vmem((36 * B, B), f32),
             vmem((2, 4 * B, 512), f32),
             vmem((W, W), f32),
@@ -610,13 +676,18 @@
             vmem((4, 2, B, 512), f32),
             vmem((2, 2, 64, 512), f32),
             vmem((2, 2, B, 512), f32),
-            dma((5, 32)), dma((5,)), dma((5, 4)), dma((5, 4)), dma((5, 8)), dma((5, 8)),
+            vmem((64, 512), f32),
+            vmem((576, B), f32),
+            dma((5, 8)), dma((5,)), dma((5,)), dma((5, 8)), dma((5, 4)), dma((5, 4)), dma((5, 8)), dma((5, 8)),
             dma((5, 4)), dma((5, 4)), dma((5, 4)), dma((5, 4)),
-            dma((2, 6)), dma((2, 6)), dma((2, 4)), dma((2, 4)), dma((5,)), dma((4,)),
+            dma((2, 6)), dma((2, 6)), dma((2, 4)), dma((2, 4)), dma((7,)), dma((4,)),
         ],
-        compiler_params=pltpu.CompilerParams(collective_id=0, has_side_effects=True),
+        compiler_params=pltpu.CompilerParams(collective_id=0, has_side_effects=True, vmem_limit_bytes=40 * 2**20),
         name="whole",
     )(past, a_cols)
+    x, z, c = (lax.axis_index(axis) for axis in ROW_COL)
+    row = (x * 16 + z * 2 + c) * 512 + lax.broadcasted_iota(jnp.int32, (512, W), 0)
+    return jnp.where(row >= lax.broadcasted_iota(jnp.int32, (512, W), 1), solved, 0.0)
 
 
 def solution(mesh):

time: 108 us -> 98.2 us (0.909)
  Pallas kernels: 104 us -> 93.7 us
  other arithmetic: 0 us -> 1.53 us
    pallas_call x1, Pallas kernels: 104 us -> 93.7 us  [body(): pl.pallas_call(whole_kernel, out_shape=jax.ShapeDtypeStruct((512, W), f32...]
    select_n x0 -> x1, other arithmetic: none -> 1.52 us  [body(): jnp.where(row >= lax.broadcasted_iota(jnp.int32, (512, W), 1), solved, 0.0)]
    unnamed x1 -> x4, local copies, waits for them, and re-layouts: 3.16 us -> 2.81 us
where the time goes in v3:
time: 98.2 us; the launch traced here: 98.1 us
  Pallas kernels  93.7 us (95%)
  local copies, waits for them, and re-layouts  2.81 us (3%)
  other arithmetic  1.53 us (2%)
    pallas_call x1, Pallas kernels, body(): pl.pallas_call(whole_kernel, out_shape=jax.ShapeDtypeStruct((512, W), f32...  93.7 us
    unnamed x4, local copies, waits for them, and re-layouts  2.81 us

profile of v3, /device:TPU:1, one launch (start us, length us, event | category | flops | bytes accessed | tf_op | source)
XLA Modules:
  0.0 98.1 jit_solution(5920221603221438177)
XLA Ops:
  0.0 0.0 copy-start
  0.0 1.6 %copy-done = f32[512,1024]{1,0:T(8,128)S(1)} copy-done((f32[512,1024]{1,0:T(8,128)S(1)}, f32[512,1024]{1,0:T(8,128)}, u32[]{:S(2)}) %copy-start) | copy-done | bytes 2097176
  1.6 0.0 copy-start.1
  1.6 1.2 %copy-done.1 = f32[512,512]{1,0:T(8,128)S(1)} copy-done((f32[512,512]{1,0:T(8,128)S(1)}, f32[512,512]{1,0:T(8,128)}, u32[]{:S(2)}) %copy-start.1) | copy-done | bytes 1048600
  2.8 93.7 %whole.1 = f32[512,1024]{1,0:T(8,128)S(1)} custom-call(f32[512,512]{1,0:T(8,128)S(1)} %copy-done.1, f32[512,1024]{1,0:T(8,128)S(1)} %copy-done), custom_call_target="tpu_custom_call" | custom-call | tf_op jit(solution)/shard_map/whole/pallas_call | solution.py:651
  96.5 1.5 %fusion = f32[512,1024]{1,0:T(8,128)} fusion(f32[512,1024]{1,0:T(8,128)S(1)} %whole.1, s32[512]{0:T(512)S(1)} %iota_add_fusion), kind=kLoop, calls=%fused_computation.1 | loop fusion | flops 1048576 | bytes 4196352 | tf_op jit(solution)/shard_map/jit(_where)/select_n | solution.py:690
  (1 shorter events, 0.0 us)
Async XLA Ops:
  0.0 1.6 %copy-start = (f32[512,1024]{1,0:T(8,128)S(1)}, f32[512,1024]{1,0:T(8,128)}, u32[]{:S(2)}) copy-start(f32[512,1024]{1,0:T(8,128)} %a_in.1) | copy-start | bytes 6291460
  1.6 1.2 %copy-start.1 = (f32[512,512]{1,0:T(8,128)S(1)}, f32[512,512]{1,0:T(8,128)}, u32[]{:S(2)}) copy-start(f32[512,512]{1,0:T(8,128)} %past_in.1) | copy-start | bytes 3145732

commit v4 on v3

--- a/solution.py
+++ b/solution.py
@@ -38,6 +38,7 @@
 STRIDE = (512, 512, 512, 768, 1024)
 SOURCE = (0, 256, 0, 512, 1280)
 SLOT = (0, 0, 0, 16, 40)
+FAR_FIRST = (4, 3, 5, 2, 6, 1, 7)
 
 
 def split(x):
@@ -166,11 +167,8 @@
         return remote(src, bundle(n, 0, width(n)), sc_send.at[n, to], bu_recv.at[n], *place, c, y)
 
     def columns_all(n):
-        def go(to, carry):
+        for to in FAR_FIRST if n < 2 else (2, 1, 3):
             column(n, to).start()
-            return carry
-
-        lax.fori_loop(1, 8 if n < 2 else 4, go, 0)
 
     def first_piece(n, on_root, k):
         return source(n, k, 1) if on_root else bundle(n, k, 1)
@@ -186,7 +184,7 @@
     def pass_on(n, on_root):
         own = pltpu.make_async_copy(first_piece(n, on_root, 0), place_of(n, me), loc.at[n])
         own.start()
-        for k in range(1, width(n)):
+        for k in (2, 1, 3) if n < 2 else FAR_FIRST:
             onward(n, on_root, k).start()
         own.wait()
 
@@ -206,11 +204,8 @@
         return remote(mine, mine, z_send.at[n, k], z_recv.at[n, z], x, lax.rem(z + k, 8), c, y)
 
     def z_start(n):
-        def go(k, carry):
+        for k in FAR_FIRST:
             z_copy(n, k).start()
-            return carry
-
-        lax.fori_loop(1, 8, go, 0)
 
     def z_wait(n):
         def wait(k, carry):
@@ -438,21 +433,23 @@
     stage_h(tiles_b)
     stage_2(rows_1)
     next_part(tiles_c)
+    stage_1(tiles_b)
     stage_5(rows_0)
     update(0)
+    stage_h(tiles_c)
     stage_2(tiles_a)
-    stage_1(tiles_b)
     stage_3(rows_1)
+    stage_y(tiles_b)
     stage_3(tiles_a)
-    stage_y(tiles_b)
-    stage_h(tiles_c)
     stage_4(rows_1)
+    stage_1(tiles_c)
+    stage_2(tiles_b)
     stage_4(tiles_a)
     update_2(0)
     stage_5(rows_1)
-    stage_2(tiles_b)
-    stage_1(tiles_c)
+    stage_y(tiles_c)
     update(1)
+    stage_3(tiles_b)
     stage_5(tiles_a)
     take(0)
 
@@ -473,20 +470,18 @@
         update_5(1)
 
     events = {
-        (0, 0): lambda: stage_3(tiles_b),
-        (0, 1): lambda: stage_y(tiles_c),
         (0, 4): lambda: stage_4(tiles_b),
+        (0, 5): lambda: stage_2(tiles_c),
         (0, 6): lambda: update_2(1),
+        (0, 7): lambda: update_3(0),
         (1, -1): stage_5b,
-        (1, 1): lambda: stage_2(tiles_c),
-        (1, 3): lambda: update_3(0),
-        (1, 7): lambda: stage_3(tiles_c),
-        (2, 4): lambda: update_3(1),
-        (2, 7): lambda: stage_4(tiles_c),
-        (3, 0): stage_5c,
-        (3, 6): lambda: update_4(0),
+        (1, 6): lambda: stage_3(tiles_c),
+        (2, 2): lambda: update_3(1),
+        (2, 6): lambda: stage_4(tiles_c),
+        (3, 2): stage_5c,
+        (3, 3): lambda: update_4(0),
         (5, 1): lambda: update_4(1),
-        (6, 5): update_5ab,
+        (6, 6): update_5ab,
         (7, 0): lambda: finish(0),
         (7, 2): lambda: finish(1),
         (7, 4): lambda: finish(2),
@@ -594,6 +589,8 @@
         def fill(t, s=s):
             if (s, t) in events:
                 events[s, t]()
+            if s == 3 and t < 2:
+                return
             n = -(-len(waiting) // (B // PANEL - t))
             for _ in range(n):
                 waiting.pop(0)()

time: 98.2 us -> 88.6 us (0.902)
  Pallas kernels: 93.7 us -> 84.1 us
    pallas_call x1, Pallas kernels: 93.7 us -> 84.1 us  [body(): pl.pallas_call(whole_kernel, out_shape=jax.ShapeDtypeStruct((512, W), f32...]
where the time goes in v4:
time: 88.6 us; the launch traced here: 88.4 us
  Pallas kernels  84.1 us (95%)
  local copies, waits for them, and re-layouts  2.81 us (3%)
  other arithmetic  1.53 us (2%)
    pallas_call x1, Pallas kernels, body(): pl.pallas_call(whole_kernel, out_shape=jax.ShapeDtypeStruct((512, W), f32...  84.1 us
    unnamed x4, local copies, waits for them, and re-layouts  2.81 us

profile of v4, /device:TPU:1, one launch (start us, length us, event | category | flops | bytes accessed | tf_op | source)
XLA Modules:
  0.0 88.4 jit_solution(7332227941025455851)
XLA Ops:
  0.0 0.0 copy-start
  0.0 1.6 %copy-done = f32[512,1024]{1,0:T(8,128)S(1)} copy-done((f32[512,1024]{1,0:T(8,128)S(1)}, f32[512,1024]{1,0:T(8,128)}, u32[]{:S(2)}) %copy-start) | copy-done | bytes 2097176
  1.6 0.0 copy-start.1
  1.6 1.2 %copy-done.1 = f32[512,512]{1,0:T(8,128)S(1)} copy-done((f32[512,512]{1,0:T(8,128)S(1)}, f32[512,512]{1,0:T(8,128)}, u32[]{:S(2)}) %copy-start.1) | copy-done | bytes 1048600
  2.8 84.1 %whole.1 = f32[512,1024]{1,0:T(8,128)S(1)} custom-call(f32[512,512]{1,0:T(8,128)S(1)} %copy-done.1, f32[512,1024]{1,0:T(8,128)S(1)} %copy-done), custom_call_target="tpu_custom_call" | custom-call | tf_op jit(solution)/shard_map/whole/pallas_call | solution.py:648
  86.9 1.5 %fusion = f32[512,1024]{1,0:T(8,128)} fusion(f32[512,1024]{1,0:T(8,128)S(1)} %whole.1, s32[512]{0:T(512)S(1)} %iota_add_fusion), kind=kLoop, calls=%fused_computation.1 | loop fusion | flops 1048576 | bytes 4196352 | tf_op jit(solution)/shard_map/jit(_where)/select_n | solution.py:687
  (1 shorter events, 0.0 us)
Async XLA Ops:
  0.0 1.6 %copy-start = (f32[512,1024]{1,0:T(8,128)S(1)}, f32[512,1024]{1,0:T(8,128)}, u32[]{:S(2)}) copy-start(f32[512,1024]{1,0:T(8,128)} %a_in.1) | copy-start | bytes 6291460
  1.6 1.2 %copy-start.1 = (f32[512,512]{1,0:T(8,128)S(1)}, f32[512,512]{1,0:T(8,128)}, u32[]{:S(2)}) copy-start(f32[512,512]{1,0:T(8,128)} %past_in.1) | copy-start | bytes 3145732

commit v5 on v4

--- a/solution.py
+++ b/solution.py
@@ -435,11 +435,11 @@
     next_part(tiles_c)
     stage_1(tiles_b)
     stage_5(rows_0)
-    update(0)
     stage_h(tiles_c)
     stage_2(tiles_a)
     stage_3(rows_1)
     stage_y(tiles_b)
+    update(0)
     stage_3(tiles_a)
     stage_4(rows_1)
     stage_1(tiles_c)

time: 88.6 us -> 88.7 us (level)
  no operation moved by 1% of the time
where the time goes in v5:
time: 88.7 us; the launch traced here: 88.5 us
  Pallas kernels  84.2 us (95%)
  local copies, waits for them, and re-layouts  2.81 us (3%)
  other arithmetic  1.53 us (2%)
    pallas_call x1, Pallas kernels, body(): pl.pallas_call(whole_kernel, out_shape=jax.ShapeDtypeStruct((512, W), f32...  84.2 us
    unnamed x4, local copies, waits for them, and re-layouts  2.81 us

profile of v5, /device:TPU:1, one launch (start us, length us, event | category | flops | bytes accessed | tf_op | source)
XLA Modules:
  0.0 88.5 jit_solution(7366110299677435638)
XLA Ops:
  0.0 0.0 copy-start
  0.0 1.6 %copy-done = f32[512,1024]{1,0:T(8,128)S(1)} copy-done((f32[512,1024]{1,0:T(8,128)S(1)}, f32[512,1024]{1,0:T(8,128)}, u32[]{:S(2)}) %copy-start) | copy-done | bytes 2097176
  1.6 0.0 copy-start.1
  1.6 1.2 %copy-done.1 = f32[512,512]{1,0:T(8,128)S(1)} copy-done((f32[512,512]{1,0:T(8,128)S(1)}, f32[512,512]{1,0:T(8,128)}, u32[]{:S(2)}) %copy-start.1) | copy-done | bytes 1048600
  2.8 84.2 %whole.1 = f32[512,1024]{1,0:T(8,128)S(1)} custom-call(f32[512,512]{1,0:T(8,128)S(1)} %copy-done.1, f32[512,1024]{1,0:T(8,128)S(1)} %copy-done), custom_call_target="tpu_custom_call" | custom-call | tf_op jit(solution)/shard_map/whole/pallas_call | solution.py:648
  87.0 1.5 %fusion = f32[512,1024]{1,0:T(8,128)} fusion(f32[512,1024]{1,0:T(8,128)S(1)} %whole.1, s32[512]{0:T(512)S(1)} %iota_add_fusion), kind=kLoop, calls=%fused_computation.1 | loop fusion | flops 1048576 | bytes 4196352 | tf_op jit(solution)/shard_map/jit(_where)/select_n | solution.py:687
  (1 shorter events, 0.0 us)
Async XLA Ops:
  0.0 1.6 %copy-start = (f32[512,1024]{1,0:T(8,128)S(1)}, f32[512,1024]{1,0:T(8,128)}, u32[]{:S(2)}) copy-start(f32[512,1024]{1,0:T(8,128)} %a_in.1) | copy-start | bytes 6291460
  1.6 1.2 %copy-start.1 = (f32[512,512]{1,0:T(8,128)S(1)}, f32[512,512]{1,0:T(8,128)}, u32[]{:S(2)}) copy-start(f32[512,512]{1,0:T(8,128)} %past_in.1) | copy-start | bytes 3145732
